TPU v7x, 128 devices: a whole 4x4x4 slice. The times are simulated.
128 devices in a mesh: gx: 16 (over y_hi, z, core), gy: 8 (over y_lo, x).
Axes of the slice: x: 4, y: 4 (y_hi: 2, y_lo: 2; y = y_hi * 2 + y_lo), z: 4, core: 2. Of those that a mesh axis runs over, the one named last changes fastest.
Arguments:
- proof: bfloat16 [2048, 256, 512], P(('gx', 'gy')), may hold values from -24 to 24
- target: bfloat16 [64, 256, 512], P('gx', 'gy'), may hold values from -6 to 6
- loading: float32 [256], replicated, may hold values from 2 to 32
Outputs:
- predicted: float32 [64, 256, 512], P('gx', 'gy')
All inputs are finite; a program needn't handle non-finite values.
Results may differ from a plain program's by a relative error of at most 0.0049.
The roundings to bfloat16 on the way count: a program that leaves them out, or rounds other values in their place, can miss the bound.
Values may be sent and summed in bfloat16 or wider, within the bound.
A program may use at most 128 MiB of HBM per device.

v0:
```python
import functools
import math

import jax
import jax.numpy as jnp
import numpy as np
from jax import lax
from jax.experimental import pallas as pl
from jax.experimental.pallas import tpu as pltpu
from jax.sharding import PartitionSpec as P

GROUPS = 8
POSITIONS = 16
PHASES = 4
CHANNELS = 16
STRIDE = 264
MESH = pl.DeviceIdType.MESH


def transform_tables(length):
    half = length // 2
    sample = np.arange(length)
    phase = ((np.arange(half)[:, None] * sample[None, :]) % length).astype(np.float32) * np.float32(
        2.0 * math.pi / length
    )
    angle = sample.astype(np.float32) * np.float32(2.0 * math.pi / length)
    window = np.float32(0.5) - np.float32(0.5) * np.cos(angle)
    forward = np.stack([window * np.cos(phase), -window * np.sin(phase)], axis=1).reshape(
        length, length
    ) * np.float32(1.0 / math.sqrt(0.375 * length))
    inverse = np.stack([np.cos(phase), -np.sin(phase)], axis=1).reshape(
        length, length
    ) * np.float32(math.sqrt(2.0 / length))
    return forward.astype(np.float32), inverse.astype(np.float32)


def split_place(gx, gy):
    core, z, yh = gx % 2, (gx // 2) % 4, gx // 8
    x, yl = gy % 4, gy // 4
    vx, vz, vy = x // 2, z // 2, yh
    ux, uz, uy = (x + vx) % 2, (z + vz) % 2, (yl + yh) % 2
    return vz * 4 + vy * 2 + vx, uz * 4 + uy * 2 + ux, core


def join_place(v, u, core):
    vx, vy, vz = v % 2, (v // 2) % 2, v // 4
    ux, uy, uz = u % 2, (u // 2) % 2, u // 4
    x = 2 * vx + (ux + vx) % 2
    z = 2 * vz + (uz + vz) % 2
    return vy * 8 + z * 2 + core, ((uy + vy) % 2) * 4 + x


def bins_of(v, u, core):
    return (u * 2 + core) * GROUPS + v, 128 + (v * 2 + core) * GROUPS + u


def nt(left, right):
    return lax.dot_general(
        left, right, (((1,), (1,)), ((), ())), preferred_element_type=jnp.float32
    )


def nn(left, right):
    return lax.dot_general(
        left, right, (((1,), (0,)), ((), ())), preferred_element_type=jnp.float32
    )


def tn(left, right):
    return lax.dot_general(
        left, right, (((0,), (0,)), ((), ())), preferred_element_type=jnp.float32
    )


def kernel(
    rho,
    tab_hbm, ttab_hbm, inv_hbm, proof_hbm, target_hbm, loading,
    out,
    tab, ttab, inv, proof, target,
    stage, xsend, xrecv, msend, mrecv, macc, tmat, tsend, trecv, rows, psend, precv,
    proof_sem, tab_sem, small_sem,
    x_send_sem, x_recv_sem, m_send_sem, m_recv_sem, t_sem, p_sem,
):
    gx, gy = lax.axis_index("gx"), lax.axis_index("gy")
    v, u, core = split_place(gx, gy)
    me = gx * 8 + gy
    group = (v, u)
    position = (u * 2 + core, v * 2 + core)

    def place_of(cls, pos):
        if cls == 0:
            return join_place(v, pos // 2, pos % 2)
        return join_place(pos // 2, u, pos % 2)

    def home_of(cls, grp):
        return join_place(grp, u, core) if cls == 0 else join_place(v, grp, core)

    def pair_of(cls, phase):
        return (group[cls] // 2 + 1 + phase) % 4

    tab_copies = []
    for block in range(2 * PHASES):
        phase, cls = block // 2, block % 2
        tab_copies.append(
            pltpu.make_async_copy(
                tab_hbm.at[cls * 4 + pair_of(cls, phase)], tab.at[block], tab_sem.at[block]
            )
        )
    for copy in tab_copies[:4]:
        copy.start()

    def proof_copy(c):
        return pltpu.make_async_copy(proof_hbm.at[c], proof.at[c], proof_sem.at[c])

    for c in range(CHANNELS):
        proof_copy(c).start()
    for copy in tab_copies[4:]:
        copy.start()
    small = [
        pltpu.make_async_copy(target_hbm, target, small_sem.at[0]),
        pltpu.make_async_copy(ttab_hbm, ttab, small_sem.at[1]),
        pltpu.make_async_copy(inv_hbm, inv, small_sem.at[2]),
    ]
    for copy in small:
        copy.start()

    barrier = pltpu.get_barrier_semaphore()

    def greet(d, carry):
        other = (me + d) % 128
        pl.semaphore_signal(
            barrier, inc=1, device_id=(other // 8, other % 8), device_id_type=MESH
        )
        return carry

    lax.fori_loop(1, 128, greet, 0)

    def spectra(half, first):
        base = half * 4

        def channel(c, carry):
            if first:
                proof_copy(c).wait()
            got = nt(tab[base : base + 4].reshape(256, 512), proof[c])
            start = pl.multiple_of(c * STRIDE, 8)
            stage[0, pl.ds(start, 256), :] = got[:, :128]
            stage[1, pl.ds(start, 256), :] = got[:, 128:]
            return carry

        lax.fori_loop(0, CHANNELS, channel, 0)

    def turn(block):
        base = (block % 4) * 64

        def one(r, carry):
            low = stage[0, pl.ds(base + r, CHANNELS, stride=STRIDE), :]
            high = stage[1, pl.ds(base + r, CHANNELS, stride=STRIDE), :]
            xsend[block * 64 + r, :, 0:128] = low.astype(jnp.bfloat16)
            xsend[block * 64 + r, :, 128:256] = high.astype(jnp.bfloat16)
            return carry

        lax.fori_loop(0, 64, one, 0, unroll=8)

    def send_block(block):
        cls = block % 2
        mine = position[cls]

        def one(d, carry):
            pos = (mine + d) % POSITIONS
            pltpu.make_async_remote_copy(
                src_ref=xsend.at[pl.ds(block * 64 + pos * 4, 4)],
                dst_ref=xrecv.at[block, :, mine],
                send_sem=x_send_sem.at[block],
                recv_sem=x_recv_sem.at[block],
                device_id=place_of(cls, pos),
                device_id_type=MESH,
            ).start()
            return carry

        lax.fori_loop(1, POSITIONS, one, 0)
        for i in range(4):
            xrecv[block, i, mine] = xsend[block * 64 + mine * 4 + i]

    for copy in tab_copies[:4]:
        copy.wait()
    spectra(0, True)
    turn(0)
    turn(1)
    pl.semaphore_wait(barrier, 127)
    send_block(0)
    send_block(1)
    turn(2)
    turn(3)
    send_block(2)
    send_block(3)
    for copy in tab_copies[4:]:
        copy.wait()
    spectra(1, False)
    for block in range(4, 8):
        turn(block)
        send_block(block)

    for copy in small:
        copy.wait()
    rows[...] = nt(ttab[...], target[...])

    def pack_rows(dst):
        def one(d, carry):
            dst[d] = rows[pl.ds(d * 4, 4), :].astype(jnp.bfloat16)
            return carry

        lax.fori_loop(0, 128, one, 0, unroll=8)

    def unpack_rows(src):
        def one(d, carry):
            rows[pl.ds(d * 4, 4), :] = src[d].astype(jnp.float32)
            return carry

        lax.fori_loop(0, 128, one, 0, unroll=8)

    def send_small(src, dst, sems):
        def one(d, carry):
            other = (me + d) % 128
            pltpu.make_async_remote_copy(
                src_ref=src.at[other],
                dst_ref=dst.at[me],
                send_sem=sems.at[0],
                recv_sem=sems.at[1],
                device_id=(other // 8, other % 8),
                device_id_type=MESH,
            ).start()
            return carry

        lax.fori_loop(1, 128, one, 0)
        dst[me] = src[me]

    def wait_bytes(view, sem):
        pltpu.make_async_copy(view, view, sem).wait()

    pack_rows(tsend)
    send_small(tsend, trecv, t_sem)

    def partial_gram(block, which):
        re = xrecv[block, which * 2].reshape(256, 256)
        im = xrecv[block, which * 2 + 1].reshape(256, 256)
        ret, imt = re.T, im.T
        return (nn(ret, re) + nn(imt, im) + (nn(ret, im) - nn(imt, re))) * (1.0 / 256.0)

    def gram_copy(block, slot, grp, cls):
        return pltpu.make_async_remote_copy(
            src_ref=msend.at[block, slot],
            dst_ref=mrecv.at[cls, group[cls]],
            send_sem=m_send_sem.at[cls],
            recv_sem=m_recv_sem.at[cls],
            device_id=home_of(cls, grp),
            device_id_type=MESH,
        )

    for block in range(8):
        phase, cls = block // 2, block % 2
        wait_bytes(xrecv.at[block, :, pl.ds(0, POSITIONS - 1)], x_recv_sem.at[block])
        if phase < PHASES - 1:
            for which in range(2):
                msend[block, which] = partial_gram(block, which).astype(jnp.bfloat16)
                gram_copy(block, which, pair_of(cls, phase) * 2 + which, cls).start()
        else:
            other = (group[cls] + 1) % 2
            msend[block, 0] = partial_gram(block, other).astype(jnp.bfloat16)
            gram_copy(block, 0, pair_of(cls, phase) * 2 + other, cls).start()
    for cls in range(2):
        macc[cls] = partial_gram(6 + cls, group[cls] % 2)

    lane = lax.broadcasted_iota(jnp.int32, (16, 128), 1) // 32
    wait_bytes(trecv.at[pl.ds(0, 127)], t_sem.at[1])
    unpack_rows(trecv)
    for i in range(4):
        blocks = [rows[pl.ds(g * 4 + i, 16, stride=32), :] for g in range(8)]
        for t in range(4):
            for tile in range(2):
                total = jnp.zeros((16, 128), jnp.float32)
                for k in range(4):
                    turned = blocks[tile * 4 + k]
                    if k != t:
                        turned = pltpu.roll(turned, (32 * (k - t)) % 128, 1)
                    total = jnp.where(lane == k, turned, total)
                tmat[
                    i // 2, (i % 2) * 64 + t * 16 : (i % 2) * 64 + t * 16 + 16,
                    tile * 128 : tile * 128 + 128,
                ] = total.astype(jnp.bfloat16)

    bins = bins_of(v, u, core)
    for cls in range(2):
        wait_bytes(mrecv.at[cls, pl.ds(0, GROUPS - 1)], m_recv_sem.at[cls])
        gram = macc[cls]
        for n in range(1, GROUPS):
            gram = gram + mrecv[cls, (group[cls] + n) % GROUPS].astype(jnp.float32)
        high = gram.astype(jnp.bfloat16)
        low = (gram - high.astype(jnp.float32)).astype(jnp.bfloat16)

        def combine(straight, turned):
            return (
                0.5 * (straight[:64] - straight[64:] + turned[:64] + turned[64:]),
                0.5 * (straight[:64] + straight[64:] - turned[:64] + turned[64:]),
            )

        left = tmat[cls]
        once_re, once_im = combine(
            nn(left, high) + nn(left, low), nt(left, high) + nt(left, low)
        )
        once = jnp.concatenate([once_re, once_im], axis=0)
        once_high = once.astype(jnp.bfloat16)
        once_low = (once - once_high.astype(jnp.float32)).astype(jnp.bfloat16)
        both = jnp.concatenate([once_high, once_low], axis=0)
        straight, turned = nn(both, high), nt(both, high)
        twice_re, twice_im = combine(
            straight[:128] + straight[128:] + nn(once_high, low),
            turned[:128] + turned[128:] + nt(once_high, low),
        )
        load = loading[bins[cls]]
        step = 1.0 / (load + rho)
        keep, take = 2.0 * step - load * step * step, step * step
        pred = (keep * once_re - take * twice_re, keep * once_im - take * twice_im)
        for part in range(2):
            for g in range(8):
                k, tile = g % 4, g // 4
                total = jnp.zeros((16, 128), jnp.float32)
                for t in range(4):
                    turned = pred[part][t * 16 : t * 16 + 16, tile * 128 : tile * 128 + 128]
                    if k != t:
                        turned = pltpu.roll(turned, (32 * (t - k)) % 128, 1)
                    total = jnp.where(lane == t, turned, total)
                rows[pl.ds(g * 4 + cls * 2 + part, 16, stride=32), :] = total

    pack_rows(psend)
    send_small(psend, precv, p_sem)
    wait_bytes(precv.at[pl.ds(0, 127)], p_sem.at[1])
    unpack_rows(precv)
    out[...] = tn(rows[...].astype(jnp.bfloat16), inv[...])

    for block in range(8):
        wait_bytes(xrecv.at[block, :, pl.ds(0, POSITIONS - 1)], x_send_sem.at[block])
    for cls in range(2):
        wait_bytes(mrecv.at[cls, pl.ds(0, GROUPS - 1)], m_send_sem.at[cls])
    wait_bytes(trecv.at[pl.ds(0, 127)], t_sem.at[0])
    wait_bytes(precv.at[pl.ds(0, 127)], p_sem.at[0])


def tables(length):
    forward, inverse = transform_tables(length)
    by_pair = (
        forward.reshape(2, POSITIONS, 4, 4, length)
        .transpose(0, 2, 1, 3, 4)
        .reshape(8, POSITIONS * 4, length)
    )
    order = []
    for device in range(128):
        for number in bins_of(*split_place(device // 8, device % 8)):
            order += [2 * number, 2 * number + 1]
    return tuple(
        jnp.asarray(table).astype(jnp.bfloat16)
        for table in (by_pair, forward[order], inverse[order])
    )


def local(proof, target, loading):
    channels, segments, length = proof.shape
    rho = (1.0 + math.sqrt(2048 / segments)) ** 2
    by_pair, by_owner, inverse = tables(length)
    bf16, f32 = jnp.bfloat16, jnp.float32
    hbm = pl.BlockSpec(memory_space=pl.ANY)
    scratch = [
        pltpu.VMEM((8, 64, 512), bf16),
        pltpu.VMEM((512, 512), bf16),
        pltpu.VMEM((512, 512), bf16),
        pltpu.VMEM((16, 256, 512), bf16),
        pltpu.VMEM((128, 512), bf16),
        pltpu.VMEM((2, CHANNELS * STRIDE, 128), f32),
        pltpu.VMEM((512, CHANNELS, 256), bf16),
        pltpu.VMEM((8, 4, POSITIONS, CHANNELS, 256), bf16),
        pltpu.VMEM((8, 2, 256, 256), bf16),
        pltpu.VMEM((2, GROUPS, 256, 256), bf16),
        pltpu.VMEM((2, 256, 256), f32),
        pltpu.VMEM((2, 128, 256), bf16),
        pltpu.VMEM((128, 4, 128), bf16),
        pltpu.VMEM((128, 4, 128), bf16),
        pltpu.VMEM((512, 128), f32),
        pltpu.VMEM((128, 4, 128), bf16),
        pltpu.VMEM((128, 4, 128), bf16),
        pltpu.SemaphoreType.DMA((CHANNELS,)),
        pltpu.SemaphoreType.DMA((8,)),
        pltpu.SemaphoreType.DMA((3,)),
        pltpu.SemaphoreType.DMA((8,)),
        pltpu.SemaphoreType.DMA((8,)),
        pltpu.SemaphoreType.DMA((2,)),
        pltpu.SemaphoreType.DMA((2,)),
        pltpu.SemaphoreType.DMA((2,)),
        pltpu.SemaphoreType.DMA((2,)),
    ]
    result = pl.pallas_call(
        functools.partial(kernel, rho),
        out_shape=jax.ShapeDtypeStruct((128, length), f32),
        in_specs=[hbm] * 5 + [pl.BlockSpec(memory_space=pltpu.SMEM)],
        out_specs=pl.BlockSpec(memory_space=pltpu.VMEM),
        scratch_shapes=scratch,
        compiler_params=pltpu.CompilerParams(
            collective_id=0, has_side_effects=True, vmem_limit_bytes=56 * 2**20
        ),
    )(by_pair, by_owner, inverse, proof, target.reshape(128, length), loading)
    return result.reshape(4, 32, length)


def solution(mesh):
    return jax.shard_map(
        local,
        mesh=mesh,
        in_specs=(P(("gx", "gy"), None, None), P("gx", "gy", None), P()),
        out_specs=P("gx", "gy", None),
        check_vma=False,
    )
```

profile of v0, /device:TPU:1, one launch (start us, length us, event | category | flops | bytes accessed | tf_op | source)
XLA Modules:
  0.0 65.1 jit_solution(2985331005616873248)
XLA Ops:
  0.0 63.4 %shard_map.64 = f32[128,512]{1,0:T(8,128)} custom-call(bf16[8,64,512]{2,1,0:T(8,128)(2,1)} %constant.11.tab_hbm, bf16[512,512]{1,0:T(8,128)(2,1)} %constant.12.ttab_hbm, bf16[512,512]{1,0:T(8,128)(2,1)} %constant.13.inv_hbm, bf16[16,256,512]{2,1,0:T(8,128)(2,1)} %proof_hbm.1, bf16[128,512]{1,0:T(8,128)(2,1)} %bitcast.3, f32[256]{0:T(256)} %loading.1), custom_call_target="tpu_custom_call" | custom-call | tf_op jit(solution)/shard_map/pallas_call | solution.py:399
  63.4 1.7 %copy.8 = f32[4,32,512]{2,1,0:T(8,128)} copy(f32[4,32,512]{2,1,0:T(8,128)} %bitcast.2) | data formatting | bytes 524288
where the time goes:
time: 65.2 us; the launch traced here: 65.1 us
  Pallas kernels  63.4 us (97%)
  local copies, waits for them, and re-layouts  1.67 us (3%)
    pallas_call x1, Pallas kernels, local(): pl.pallas_call(functools.partial(kernel, rho), out_shape=jax.ShapeDtypeSt...  63.4 us
    unnamed x1, local copies, waits for them, and re-layouts  1.67 us

commit v1 on v0

v1 whole, which is shorter than its diff:
```python
import functools
import math

import jax
import jax.numpy as jnp
import numpy as np
from jax import lax
from jax.experimental import pallas as pl
from jax.experimental.pallas import tpu as pltpu
from jax.sharding import PartitionSpec as P

GROUPS = 8
POSITIONS = 16
CHANNELS = 16
STRIDE = 520
OTHERS = (2, 4, 8, 14, 3, 5, 9, 15, 6, 12, 10, 7, 13, 11, 1)
PIECE = 128
ORDERS = ((4, 2, 1), (1, 2, 4))
MESH = pl.DeviceIdType.MESH


def transform_tables(length):
    half = length // 2
    sample = np.arange(length)
    phase = ((np.arange(half)[:, None] * sample[None, :]) % length).astype(np.float32) * np.float32(
        2.0 * math.pi / length
    )
    angle = sample.astype(np.float32) * np.float32(2.0 * math.pi / length)
    window = np.float32(0.5) - np.float32(0.5) * np.cos(angle)
    forward = np.stack([window * np.cos(phase), -window * np.sin(phase)], axis=1).reshape(
        length, length
    ) * np.float32(1.0 / math.sqrt(0.375 * length))
    inverse = np.stack([np.cos(phase), -np.sin(phase)], axis=1).reshape(
        length, length
    ) * np.float32(math.sqrt(2.0 / length))
    return forward.astype(np.float32), inverse.astype(np.float32)


def split_place(gx, gy):
    core, z, yh = gx % 2, (gx // 2) % 4, gx // 8
    x, yl = gy % 4, gy // 4
    v = (z // 2, yh, x // 2)
    return v, ((z + v[0]) % 2, (yl + yh) % 2, (x + v[2]) % 2), core


def number(bits):
    return (bits[0] * 2 + bits[1]) * 2 + bits[2]


def bins_of(v, u, core):
    return (
        (number(u) * 2 + core) * GROUPS + number(v),
        128 + (number(v) * 2 + core) * GROUPS + number(u),
    )


def next_bit(offset, piece):
    return next(bit for bit in ORDERS[piece] if offset & bit)


def feeders(offset, piece):
    return [
        other for other in range(1, GROUPS) if other ^ next_bit(other, piece) == offset
    ]


def nt(left, right):
    return lax.dot_general(
        left, right, (((1,), (1,)), ((), ())), preferred_element_type=jnp.float32
    )


def nn(left, right):
    return lax.dot_general(
        left, right, (((1,), (0,)), ((), ())), preferred_element_type=jnp.float32
    )


def tn(left, right):
    return lax.dot_general(
        left, right, (((0,), (0,)), ((), ())), preferred_element_type=jnp.float32
    )


def kernel(
    rho,
    tab_hbm, ttab_hbm, proof_hbm, target_hbm, loading,
    out,
    tab, ttab, proof, target,
    stage, xsend, xrecv, xlast, part, msend, mrecv, tmat, tsend, tpass, trecv, rows, psend, precv,
    proof_sem, tab_sem, small_sem,
    x_send_sem, x_recv_sem, m_send_sem, m_recv_sem, t_sem, p_sem,
):
    gx, gy = lax.axis_index("gx"), lax.axis_index("gy")
    v, u, core = split_place(gx, gy)
    group = (v, u)
    mine = (number(u) * 2 + core, number(v) * 2 + core)

    z, yh, x, yl = (gx // 2) % 4, gx // 8, gy % 4, gy // 4
    z_flip = (2 * v[0] + 1 - z % 2, 2 * (1 - v[0]) + 1 - z % 2)
    x_flip = (2 * v[2] + 1 - x % 2, 2 * (1 - v[2]) + 1 - x % 2)
    yh_flip = (yh, 1 - yh)

    def place(which, offset, flip_core=0):
        there_z = z_flip[which] if offset & 4 else z
        there_yh = yh_flip[which] if offset & 2 else yh
        there_yl = 1 - yl if offset & 2 else yl
        there_x = x_flip[which] if offset & 1 else x
        there_core = 1 - core if flip_core else core
        return there_yh * 8 + there_z * 2 + there_core, there_yl * 4 + there_x

    def flipped(bit, flip):
        return 1 - bit if flip else bit

    def pos_at(cls, offset):
        bits = (u, v)[cls]
        return (
            number([flipped(b, offset & (8 >> n)) for n, b in enumerate(bits)]) * 2
            + flipped(core, offset & 1)
        )

    def pair_at(cls, offset):
        bits = group[cls]
        return flipped(bits[0], offset & 2) * 2 + flipped(bits[1], offset & 1)

    barrier = pltpu.get_barrier_semaphore()

    def tab_copy(block):
        cls, offset = block % 2, 3 - block // 2
        return pltpu.make_async_copy(
            tab_hbm.at[cls * 4 + pair_at(cls, offset)], tab.at[block], tab_sem.at[block]
        )

    def proof_copy(c):
        return pltpu.make_async_copy(proof_hbm.at[c], proof.at[c], proof_sem.at[c])

    for block in range(2):
        tab_copy(block).start()
    for c in range(CHANNELS):
        proof_copy(c).start()
    for block in range(2, 8):
        tab_copy(block).start()
    small = [
        pltpu.make_async_copy(target_hbm, target, small_sem.at[0]),
        pltpu.make_async_copy(ttab_hbm, ttab, small_sem.at[1]),
    ]
    for copy in small:
        copy.start()

    for other in OTHERS:
        for cls in range(2):
            pl.semaphore_signal(
                barrier, inc=1, device_id=place(cls, other // 2, other % 2), device_id_type=MESH
            )
    tab_copy(0).wait()
    tab_copy(1).wait()

    def spectra(begin, end, channels):
        lines = tab[begin:end].reshape((end - begin) * 64, 512)
        for c in channels:
            got = nt(lines, proof[c])
            start = c * STRIDE + begin * 64
            stage[0, start : start + (end - begin) * 64, :] = got[:, :128]
            stage[1, start : start + (end - begin) * 64, :] = got[:, 128:]

    def turn(block):
        def one(n, carry):
            for i in range(4):
                row = block * 64 + n * 4 + i
                low = stage[0, pl.ds(row, CHANNELS, stride=STRIDE), :]
                high = stage[1, pl.ds(row, CHANNELS, stride=STRIDE), :]
                xsend[row, :, 0:128] = low.astype(jnp.bfloat16)
                xsend[row, :, 128:256] = high.astype(jnp.bfloat16)
            return carry

        lax.fori_loop(0, POSITIONS, one, 0, unroll=4)

    def send_pair(offset, classes=(0, 1)):
        slot = 3 - offset
        base = [(slot * 2 + cls) * 64 for cls in range(2)]
        for other in OTHERS:
            for cls in classes:
                pltpu.make_async_remote_copy(
                    src_ref=xsend.at[pl.ds(base[cls] + pos_at(cls, other) * 4, 4)],
                    dst_ref=xrecv.at[cls, slot, :, mine[cls]],
                    send_sem=x_send_sem.at[cls, slot],
                    recv_sem=x_recv_sem.at[cls, slot],
                    device_id=place(cls, other // 2, other % 2),
                    device_id_type=MESH,
                ).start()
        for cls in classes:
            for i in range(4):
                xrecv[cls, slot, i, mine[cls]] = xsend[base[cls] + mine[cls] * 4 + i]

    def send_last(offset, classes=(0, 1)):
        slot = 1 - offset
        base = [
            (6 + cls) * 64 + flipped(group[cls][2], offset) * 2 for cls in range(2)
        ]
        for other in OTHERS:
            for cls in classes:
                pltpu.make_async_remote_copy(
                    src_ref=xsend.at[pl.ds(base[cls] + pos_at(cls, other) * 4, 2)],
                    dst_ref=xlast.at[cls, slot, :, mine[cls]],
                    send_sem=x_send_sem.at[cls, 3 + slot],
                    recv_sem=x_recv_sem.at[cls, 3 + slot],
                    device_id=place(cls, other // 2, other % 2),
                    device_id_type=MESH,
                ).start()
        for cls in classes:
            for i in range(2):
                xlast[cls, slot, i, mine[cls]] = xsend[base[cls] + mine[cls] * 4 + i]

    def wait_bytes(view, sem):
        pltpu.make_async_copy(view, view, sem).wait()

    for c in range(8):
        proof_copy(c).wait()
    spectra(0, 2, range(8))
    for c in range(8, CHANNELS):
        proof_copy(c).wait()
    spectra(0, 2, range(8, CHANNELS))
    turn(0)
    turn(1)
    pl.semaphore_wait(barrier, 2 * len(OTHERS))
    send_pair(3)
    for block in range(2, 8):
        tab_copy(block).wait()
    spectra(2, 8, range(CHANNELS))
    turn(2)
    turn(3)
    send_pair(2)
    for block in range(4, 8):
        turn(block)

    for copy in small:
        copy.wait()
    rows[...] = nt(ttab[...], target[...])

    def along_positions(src, dst, sems):
        for other in OTHERS:
            pltpu.make_async_remote_copy(
                src_ref=src(pos_at(0, other)),
                dst_ref=dst(mine[0]),
                send_sem=sems.at[0],
                recv_sem=sems.at[1],
                device_id=place(0, other // 2, other % 2),
                device_id_type=MESH,
            ).start()

    def along_groups(src, dst, sems):
        here = number(v)
        for offset in range(1, GROUPS):
            there = number([flipped(bit, offset & (4 >> n)) for n, bit in enumerate(v)])
            pltpu.make_async_remote_copy(
                src_ref=src.at[there],
                dst_ref=dst.at[here],
                send_sem=sems.at[0],
                recv_sem=sems.at[1],
                device_id=place(1, offset),
                device_id_type=MESH,
            ).start()
        dst[here] = src[here]

    for pos in range(POSITIONS):
        for grp in range(GROUPS):
            at = (pos * GROUPS + grp) * 4
            tsend[pos, grp] = rows[at : at + 4, :].astype(jnp.bfloat16)
    along_positions(lambda p: tsend.at[p], lambda p: tpass.at[:, p], t_sem.at[0])
    for grp in range(GROUPS):
        tpass[grp, mine[0]] = tsend[mine[0], grp]

    def gram(re, im):
        re, im = re.reshape(256, 256), im.reshape(256, 256)
        ret, imt = re.T, im.T
        return (nn(ret, re) + nn(imt, im) + (nn(ret, im) - nn(imt, re))) * (1.0 / 256.0)

    def pair_grams(cls, offset):
        slot = 3 - offset
        wait_bytes(xrecv.at[cls, slot, :, pl.ds(0, POSITIONS - 1)], x_recv_sem.at[cls, slot])
        for bit in (1, 0):
            row = flipped(group[cls][2], bit) * 2
            part[cls, offset * 2 + bit] = gram(
                xrecv[cls, slot, row], xrecv[cls, slot, row + 1]
            )

    def last_gram(cls, offset):
        slot = 1 - offset
        wait_bytes(xlast.at[cls, slot, :, pl.ds(0, POSITIONS - 1)], x_recv_sem.at[cls, 3 + slot])
        part[cls, offset] = gram(xlast[cls, slot, 0], xlast[cls, slot, 1])

    def gram_sum(cls, offset, piece):
        total = part[cls, offset, pl.ds(piece * PIECE, PIECE), :]
        for other in feeders(offset, piece):
            wait_bytes(mrecv.at[cls, piece, other], m_recv_sem.at[cls, piece, other])
            total = total + mrecv[cls, piece, other].astype(jnp.float32)
        return total

    def pass_on(cls, offset, piece):
        msend[cls, piece, offset] = gram_sum(cls, offset, piece).astype(jnp.bfloat16)
        pltpu.make_async_remote_copy(
            src_ref=msend.at[cls, piece, offset],
            dst_ref=mrecv.at[cls, piece, offset],
            send_sem=m_send_sem.at[cls, piece, offset],
            recv_sem=m_recv_sem.at[cls, piece, offset],
            device_id=place(1 - cls, next_bit(offset, piece)),
            device_id_type=MESH,
        ).start()

    for cls in range(2):
        pair_grams(cls, 3)
        pass_on(cls, 7, 0)
        pass_on(cls, 7, 1)
        pass_on(cls, 6, 0)
        send_pair(1, (cls,))
    for cls in range(2):
        pair_grams(cls, 2)
        pass_on(cls, 5, 0)
        pass_on(cls, 5, 1)
        pass_on(cls, 4, 0)
        send_last(1, (cls,))
    wait_bytes(tpass.at[:, pl.ds(0, POSITIONS - 1)], t_sem.at[0, 1])
    along_groups(tpass, trecv, t_sem.at[1])
    for cls in range(2):
        pass_on(cls, 6, 1)
    for cls in range(2):
        pair_grams(cls, 1)
        pass_on(cls, 3, 0)
        pass_on(cls, 3, 1)
        pass_on(cls, 2, 0)
        send_last(0, (cls,))
    for cls in range(2):
        pass_on(cls, 4, 1)
    for cls in range(2):
        last_gram(cls, 1)
        pass_on(cls, 1, 0)
        pass_on(cls, 1, 1)
    for cls in range(2):
        pass_on(cls, 2, 1)

    lane = lax.broadcasted_iota(jnp.int32, (16, 128), 1) // 32
    wait_bytes(trecv.at[pl.ds(0, GROUPS - 1)], t_sem.at[1, 1])
    for device in range(128):
        bits_v, bits_u, its_core = split_place(device // 8, device % 8)
        rows[device * 4 : device * 4 + 4, :] = trecv[
            number(bits_v), number(bits_u) * 2 + its_core
        ].astype(jnp.float32)
    for i in range(4):
        blocks = [rows[pl.ds(g * 4 + i, 16, stride=32), :] for g in range(8)]
        for t in range(4):
            for tile in range(2):
                total = jnp.zeros((16, 128), jnp.float32)
                for k in range(4):
                    turned = blocks[tile * 4 + k]
                    if k != t:
                        turned = pltpu.roll(turned, (32 * (k - t)) % 128, 1)
                    total = jnp.where(lane == k, turned, total)
                tmat[
                    i // 2, (i % 2) * 64 + t * 16 : (i % 2) * 64 + t * 16 + 16,
                    tile * 128 : tile * 128 + 128,
                ] = total.astype(jnp.bfloat16)

    for cls in range(2):
        last_gram(cls, 0)

    bins = bins_of(v, u, core)
    for cls in range(2):
        total = jnp.concatenate([gram_sum(cls, 0, piece) for piece in range(2)], axis=0)
        high = total.astype(jnp.bfloat16)
        low = (total - high.astype(jnp.float32)).astype(jnp.bfloat16)

        def combine(straight, turned):
            return (
                0.5 * (straight[:64] - straight[64:] + turned[:64] + turned[64:]),
                0.5 * (straight[:64] + straight[64:] - turned[:64] + turned[64:]),
            )

        left = tmat[cls]
        once_re, once_im = combine(
            nn(left, high) + nn(left, low), nt(left, high) + nt(left, low)
        )
        once = jnp.concatenate([once_re, once_im], axis=0)
        once_high = once.astype(jnp.bfloat16)
        once_low = (once - once_high.astype(jnp.float32)).astype(jnp.bfloat16)
        both = jnp.concatenate([once_high, once_low], axis=0)
        straight, turned = nn(both, high), nt(both, high)
        twice_re, twice_im = combine(
            straight[:128] + straight[128:] + nn(once_high, low),
            turned[:128] + turned[128:] + nt(once_high, low),
        )
        load = loading[bins[cls]]
        step = 1.0 / (load + rho)
        keep, take = 2.0 * step - load * step * step, step * step
        pred = (keep * once_re - take * twice_re, keep * once_im - take * twice_im)
        for side in range(2):
            for g in range(8):
                k, tile = g % 4, g // 4
                moved = jnp.zeros((16, 128), jnp.float32)
                for t in range(4):
                    turned = pred[side][t * 16 : t * 16 + 16, tile * 128 : tile * 128 + 128]
                    if k != t:
                        turned = pltpu.roll(turned, (32 * (t - k)) % 128, 1)
                    moved = jnp.where(lane == t, turned, moved)
                rows[pl.ds(g * 4 + cls * 2 + side, 16, stride=32), :] = moved

    me = gx * 8 + gy
    for device in range(128):
        psend[device] = rows[device * 4 : device * 4 + 4, :].astype(jnp.bfloat16)
    columns = [(gy + n) % 8 for n in range(8)]

    def give(row, column):
        pltpu.make_async_remote_copy(
            src_ref=psend.at[row * 8 + column],
            dst_ref=precv.at[me],
            send_sem=p_sem.at[0],
            recv_sem=p_sem.at[1],
            device_id=(row, column),
            device_id_type=MESH,
        ).start()

    def give_line(n, carry):
        for column in columns:
            give((gx + n) % 16, column)
        return carry

    lax.fori_loop(1, 16, give_line, 0)
    for column in columns[1:]:
        give(gx, column)
    precv[me] = psend[me]
    wait_bytes(precv.at[pl.ds(0, 127)], p_sem.at[1])
    for device in range(128):
        rows[device * 4 : device * 4 + 4, :] = precv[device].astype(jnp.float32)
    out[...] = rows[...].astype(jnp.bfloat16)

    for cls in range(2):
        for slot in range(3):
            wait_bytes(xrecv.at[cls, slot, :, pl.ds(0, POSITIONS - 1)], x_send_sem.at[cls, slot])
        for slot in range(2):
            wait_bytes(xlast.at[cls, slot, :, pl.ds(0, POSITIONS - 1)], x_send_sem.at[cls, 3 + slot])
        for piece in range(2):
            for offset in range(1, GROUPS):
                wait_bytes(msend.at[cls, piece, offset], m_send_sem.at[cls, piece, offset])
    wait_bytes(tpass.at[:, pl.ds(0, POSITIONS - 1)], t_sem.at[0, 0])
    wait_bytes(trecv.at[pl.ds(0, GROUPS - 1)], t_sem.at[1, 0])
    wait_bytes(precv.at[pl.ds(0, 127)], p_sem.at[0])


def tables(length):
    forward, inverse = transform_tables(length)
    by_pair = (
        forward.reshape(2, POSITIONS, 4, 4, length)
        .transpose(0, 2, 1, 3, 4)
        .reshape(8, POSITIONS * 4, length)
    )
    first = []
    bits = [(n // 4, n // 2 % 2, n % 2) for n in range(GROUPS)]
    for pos in range(POSITIONS):
        for grp in range(GROUPS):
            for found in bins_of(bits[grp], bits[pos // 2], pos % 2):
                first += [2 * found, 2 * found + 1]
    second = []
    for device in range(128):
        for found in bins_of(*split_place(device // 8, device % 8)):
            second += [2 * found, 2 * found + 1]
    return tuple(
        jnp.asarray(table).astype(jnp.bfloat16)
        for table in (by_pair, forward[first], inverse[second])
    )


def local(proof, target, loading):
    channels, segments, length = proof.shape
    rho = (1.0 + math.sqrt(2048 / segments)) ** 2
    by_pair, by_owner, inverse = tables(length)
    bf16, f32 = jnp.bfloat16, jnp.float32
    hbm = pl.BlockSpec(memory_space=pltpu.HBM)
    scratch = [
        pltpu.VMEM((8, 64, 512), bf16),
        pltpu.VMEM((512, 512), bf16),
        pltpu.VMEM((16, 256, 512), bf16),
        pltpu.VMEM((128, 512), bf16),
        pltpu.VMEM((2, CHANNELS * STRIDE, 128), f32),
        pltpu.VMEM((512, CHANNELS, 256), bf16),
        pltpu.VMEM((2, 3, 4, POSITIONS, CHANNELS, 256), bf16),
        pltpu.VMEM((2, 2, 2, POSITIONS, CHANNELS, 256), bf16),
        pltpu.VMEM((2, GROUPS, 256, 256), f32),
        pltpu.VMEM((2, 2, GROUPS, PIECE, 256), bf16),
        pltpu.VMEM((2, 2, GROUPS, PIECE, 256), bf16),
        pltpu.VMEM((2, 128, 256), bf16),
        pltpu.VMEM((POSITIONS, GROUPS, 4, 128), bf16),
        pltpu.VMEM((GROUPS, POSITIONS, 4, 128), bf16),
        pltpu.VMEM((GROUPS, POSITIONS, 4, 128), bf16),
        pltpu.VMEM((512, 128), f32),
        pltpu.VMEM((128, 4, 128), bf16),
        pltpu.VMEM((128, 4, 128), bf16),
        pltpu.SemaphoreType.DMA((CHANNELS,)),
        pltpu.SemaphoreType.DMA((8,)),
        pltpu.SemaphoreType.DMA((2,)),
        pltpu.SemaphoreType.DMA((2, 5)),
        pltpu.SemaphoreType.DMA((2, 5)),
        pltpu.SemaphoreType.DMA((2, 2, GROUPS)),
        pltpu.SemaphoreType.DMA((2, 2, GROUPS)),
        pltpu.SemaphoreType.DMA((2, 2)),
        pltpu.SemaphoreType.DMA((2,)),
    ]
    hold = [
        pltpu.with_memory_space_constraint(array, pltpu.HBM)
        for array in (by_pair, by_owner, proof, target.reshape(128, length))
    ]
    spectra = pl.pallas_call(
        functools.partial(kernel, rho),
        out_shape=jax.ShapeDtypeStruct((512, 128), bf16),
        in_specs=[hbm] * 4 + [pl.BlockSpec(memory_space=pltpu.SMEM)],
        out_specs=pl.BlockSpec(memory_space=pltpu.VMEM),
        scratch_shapes=scratch,
        compiler_params=pltpu.CompilerParams(
            collective_id=0, has_side_effects=True, vmem_limit_bytes=40 * 2**20
        ),
    )(*hold, loading)
    return tn(spectra, inverse).reshape(4, 32, length)


def solution(mesh):
    return jax.shard_map(
        local,
        mesh=mesh,
        in_specs=(P(("gx", "gy"), None, None), P("gx", "gy", None), P()),
        out_specs=P("gx", "gy", None),
        check_vma=False,
    )
```

time: 65.2 us -> 55.2 us (0.85)
  Pallas kernels: 63.4 us -> 53.5 us
  local copies, waits for them, and re-layouts: 1.67 us -> 0.68 us
  matrix products: 0 us -> 0.96 us
    pallas_call x1, Pallas kernels: 63.4 us -> 53.5 us  [local(): pl.pallas_call(functools.partial(kernel, rho), out_shape=jax.ShapeDtypeSt...]
    unnamed x1 -> x4, local copies, waits for them, and re-layouts: 1.67 us -> 0.68 us
    dot_general x0 -> x1, matrix products: none -> 0.96 us  [tn(): lax.dot_general(left, right, (((0,), (0,)), ((), ())), preferred_element_...]
where the time goes in v1:
time: 55.2 us; the launch traced here: 55.1 us
  Pallas kernels  53.5 us (97%)
  matrix products  0.96 us (2%)
  local copies, waits for them, and re-layouts  0.68 us (1%)
    pallas_call x1, Pallas kernels, local(): pl.pallas_call(functools.partial(kernel, rho), out_shape=jax.ShapeDtypeSt...  53.5 us

profile of v1, /device:TPU:1, one launch (start us, length us, event | category | flops | bytes accessed | tf_op | source)
XLA Modules:
  0.0 55.1 jit_solution(15611271018485100420)
XLA Ops:
  0.0 0.0 copy-start
  0.0 0.7 %copy-done = f32[256]{0:T(256)S(1)} copy-done((f32[256]{0:T(256)S(1)}, f32[256]{0:T(256)}, u32[]{:S(2)}) %copy-start) | copy-done | bytes 1048
  0.7 0.0 copy-start.1
  0.7 53.5 %shard_map.64 = bf16[512,128]{1,0:T(8,128)(2,1)S(1)} custom-call(bf16[8,64,512]{2,1,0:T(8,128)(2,1)} %constant.11.tab_hbm, bf16[512,512]{1,0:T(8,128)(2,1)} %constant.12.ttab_hbm, bf16[16,256,512]{2,1,0:T(8,128)(2,1)} %proof_hbm.1, bf16[128,512]{1,0:T(8,128)(2,1)} %bitcast.4, f32[256]{0:T(256)S(1)} %copy-done), custom_call_target="tpu_custom_call" | custom-call | tf_op jit(solution)/shard_map/pallas_call | solution.py:510
  54.1 0.0 copy-done.1
  54.2 1.0 %fusion = f32[128,512]{1,0:T(8,128)} fusion(bf16[512,128]{1,0:T(8,128)(2,1)S(1)} %shard_map.64, bf16[512,512]{1,0:T(8,128)(2,1)S(1)} %copy-done.1), kind=kOutput, calls=%fused_computation | convolution fusion | flops 67108864 | bytes 917504 | tf_op jit(solution)/shard_map/dot_general | solution.py:80
Async XLA Ops:
  0.0 0.7 %copy-start = (f32[256]{0:T(256)S(1)}, f32[256]{0:T(256)}, u32[]{:S(2)}) copy-start(f32[256]{0:T(256)} %loading.1) | copy-start | bytes 3076
  0.7 53.5 %copy-start.1 = (bf16[512,512]{1,0:T(8,128)(2,1)S(1)}, bf16[512,512]{1,0:T(8,128)(2,1)}, u32[]{:S(2)}) copy-start(bf16[512,512]{1,0:T(8,128)(2,1)} %constant.13) | copy-start | bytes 1572868

commit v2 on v1

--- a/solution.py
+++ b/solution.py
@@ -14,8 +14,12 @@
 CHANNELS = 16
 STRIDE = 520
 OTHERS = (2, 4, 8, 14, 3, 5, 9, 15, 6, 12, 10, 7, 13, 11, 1)
+FAR_FIRST = sorted(
+    ((v, u, core) for v in range(8) for u in range(8) for core in range(2) if v or u or core),
+    key=lambda way: -(way[0].bit_count() + way[1].bit_count()),
+)
 PIECE = 128
-ORDERS = ((4, 2, 1), (1, 2, 4))
+ORDERS = ((2, 4, 1), (1, 4, 2))
 MESH = pl.DeviceIdType.MESH
 
 
@@ -84,9 +88,9 @@
 
 def kernel(
     rho,
-    tab_hbm, ttab_hbm, proof_hbm, target_hbm, loading,
+    tab_hbm, ttab_hbm, proof_hbm, target_hbm, loading_hbm,
     out,
-    tab, ttab, proof, target,
+    tab, ttab, proof, target, loading,
     stage, xsend, xrecv, xlast, part, msend, mrecv, tmat, tsend, tpass, trecv, rows, psend, precv,
     proof_sem, tab_sem, small_sem,
     x_send_sem, x_recv_sem, m_send_sem, m_recv_sem, t_sem, p_sem,
@@ -97,17 +101,21 @@
     mine = (number(u) * 2 + core, number(v) * 2 + core)
 
     z, yh, x, yl = (gx // 2) % 4, gx // 8, gy % 4, gy // 4
-    z_flip = (2 * v[0] + 1 - z % 2, 2 * (1 - v[0]) + 1 - z % 2)
-    x_flip = (2 * v[2] + 1 - x % 2, 2 * (1 - v[2]) + 1 - x % 2)
-    yh_flip = (yh, 1 - yh)
-
-    def place(which, offset, flip_core=0):
-        there_z = z_flip[which] if offset & 4 else z
-        there_yh = yh_flip[which] if offset & 2 else yh
-        there_yl = 1 - yl if offset & 2 else yl
-        there_x = x_flip[which] if offset & 1 else x
+    z_flip = (2 * v[0] + 1 - z % 2, 2 * (1 - v[0]) + 1 - z % 2, 2 * (1 - v[0]) + z % 2)
+    x_flip = (2 * v[2] + 1 - x % 2, 2 * (1 - v[2]) + 1 - x % 2, 2 * (1 - v[2]) + x % 2)
+
+    def place_off(by_v, by_u, flip_core=0):
+        turns_z = (z, z_flip[0], z_flip[1], z_flip[2])
+        turns_x = (x, x_flip[0], x_flip[1], x_flip[2])
+        there_z = turns_z[(by_v >> 2 & 1) * 2 + (by_u >> 2 & 1)]
+        there_x = turns_x[(by_v & 1) * 2 + (by_u & 1)]
+        there_yh = 1 - yh if by_v & 2 else yh
+        there_yl = 1 - yl if (by_v ^ by_u) & 2 else yl
         there_core = 1 - core if flip_core else core
         return there_yh * 8 + there_z * 2 + there_core, there_yl * 4 + there_x
+
+    def place(which, offset, flip_core=0):
+        return place_off(*((0, offset) if which == 0 else (offset, 0)), flip_core)
 
     def flipped(bit, flip):
         return 1 - bit if flip else bit
@@ -143,6 +151,7 @@
     small = [
         pltpu.make_async_copy(target_hbm, target, small_sem.at[0]),
         pltpu.make_async_copy(ttab_hbm, ttab, small_sem.at[1]),
+        pltpu.make_async_copy(loading_hbm, loading, small_sem.at[2]),
     ]
     for copy in small:
         copy.start()
@@ -192,18 +201,19 @@
             for i in range(4):
                 xrecv[cls, slot, i, mine[cls]] = xsend[base[cls] + mine[cls] * 4 + i]
 
-    def send_last(offset, classes=(0, 1)):
-        slot = 1 - offset
+    def send_single(offset, classes=(0, 1)):
+        slot = 3 - offset
         base = [
-            (6 + cls) * 64 + flipped(group[cls][2], offset) * 2 for cls in range(2)
+            ((3 - offset // 2) * 2 + cls) * 64 + flipped(group[cls][2], offset % 2) * 2
+            for cls in range(2)
         ]
         for other in OTHERS:
             for cls in classes:
                 pltpu.make_async_remote_copy(
                     src_ref=xsend.at[pl.ds(base[cls] + pos_at(cls, other) * 4, 2)],
                     dst_ref=xlast.at[cls, slot, :, mine[cls]],
-                    send_sem=x_send_sem.at[cls, 3 + slot],
-                    recv_sem=x_recv_sem.at[cls, 3 + slot],
+                    send_sem=x_send_sem.at[cls, 2 + slot],
+                    recv_sem=x_recv_sem.at[cls, 2 + slot],
                     device_id=place(cls, other // 2, other % 2),
                     device_id_type=MESH,
                 ).start()
@@ -213,29 +223,6 @@
 
     def wait_bytes(view, sem):
         pltpu.make_async_copy(view, view, sem).wait()
-
-    for c in range(8):
-        proof_copy(c).wait()
-    spectra(0, 2, range(8))
-    for c in range(8, CHANNELS):
-        proof_copy(c).wait()
-    spectra(0, 2, range(8, CHANNELS))
-    turn(0)
-    turn(1)
-    pl.semaphore_wait(barrier, 2 * len(OTHERS))
-    send_pair(3)
-    for block in range(2, 8):
-        tab_copy(block).wait()
-    spectra(2, 8, range(CHANNELS))
-    turn(2)
-    turn(3)
-    send_pair(2)
-    for block in range(4, 8):
-        turn(block)
-
-    for copy in small:
-        copy.wait()
-    rows[...] = nt(ttab[...], target[...])
 
     def along_positions(src, dst, sems):
         for other in OTHERS:
@@ -262,6 +249,27 @@
             ).start()
         dst[here] = src[here]
 
+    for begin, end in ((0, 4), (4, 8), (8, CHANNELS)):
+        for c in range(begin, end):
+            proof_copy(c).wait()
+        spectra(0, 2, range(begin, end))
+    turn(0)
+    pl.semaphore_wait(barrier, 2 * len(OTHERS))
+    send_pair(3, (0,))
+    turn(1)
+    send_pair(3, (1,))
+    for block in range(2, 8):
+        tab_copy(block).wait()
+    spectra(2, 8, range(CHANNELS))
+    turn(2)
+    turn(3)
+    send_pair(2)
+    turn(4)
+    turn(5)
+    for copy in small:
+        copy.wait()
+    rows[...] = nt(ttab[...], target[...])
+
     for pos in range(POSITIONS):
         for grp in range(GROUPS):
             at = (pos * GROUPS + grp) * 4
@@ -269,6 +277,10 @@
     along_positions(lambda p: tsend.at[p], lambda p: tpass.at[:, p], t_sem.at[0])
     for grp in range(GROUPS):
         tpass[grp, mine[0]] = tsend[mine[0], grp]
+
+    send_single(3)
+    turn(6)
+    turn(7)
 
     def gram(re, im):
         re, im = re.reshape(256, 256), im.reshape(256, 256)
@@ -284,19 +296,28 @@
                 xrecv[cls, slot, row], xrecv[cls, slot, row + 1]
             )
 
-    def last_gram(cls, offset):
-        slot = 1 - offset
-        wait_bytes(xlast.at[cls, slot, :, pl.ds(0, POSITIONS - 1)], x_recv_sem.at[cls, 3 + slot])
+    def single_gram(cls, offset):
+        slot = 3 - offset
+        wait_bytes(xlast.at[cls, slot, :, pl.ds(0, POSITIONS - 1)], x_recv_sem.at[cls, 2 + slot])
         part[cls, offset] = gram(xlast[cls, slot, 0], xlast[cls, slot, 1])
+
+    def wait_fed(cls, offset, piece):
+        for other in feeders(offset, piece):
+            wait_bytes(mrecv.at[cls, piece, other], m_recv_sem.at[cls, piece, other])
+
+    def wait_sums(offset):
+        for cls in range(2):
+            for piece in range(2):
+                wait_fed(cls, offset, piece)
 
     def gram_sum(cls, offset, piece):
         total = part[cls, offset, pl.ds(piece * PIECE, PIECE), :]
         for other in feeders(offset, piece):
-            wait_bytes(mrecv.at[cls, piece, other], m_recv_sem.at[cls, piece, other])
             total = total + mrecv[cls, piece, other].astype(jnp.float32)
         return total
 
     def pass_on(cls, offset, piece):
+        wait_fed(cls, offset, piece)
         msend[cls, piece, offset] = gram_sum(cls, offset, piece).astype(jnp.bfloat16)
         pltpu.make_async_remote_copy(
             src_ref=msend.at[cls, piece, offset],
@@ -309,32 +330,34 @@
 
     for cls in range(2):
         pair_grams(cls, 3)
+        pass_on(cls, 7, 1)
         pass_on(cls, 7, 0)
-        pass_on(cls, 7, 1)
         pass_on(cls, 6, 0)
-        send_pair(1, (cls,))
+    send_single(2)
     for cls in range(2):
         pair_grams(cls, 2)
-        pass_on(cls, 5, 0)
         pass_on(cls, 5, 1)
-        pass_on(cls, 4, 0)
-        send_last(1, (cls,))
+    send_single(1)
     wait_bytes(tpass.at[:, pl.ds(0, POSITIONS - 1)], t_sem.at[0, 1])
     along_groups(tpass, trecv, t_sem.at[1])
     for cls in range(2):
         pass_on(cls, 6, 1)
     for cls in range(2):
-        pair_grams(cls, 1)
+        pass_on(cls, 5, 0)
+        pass_on(cls, 4, 0)
+    for cls in range(2):
+        single_gram(cls, 3)
+        single_gram(cls, 2)
+        pass_on(cls, 3, 1)
         pass_on(cls, 3, 0)
-        pass_on(cls, 3, 1)
         pass_on(cls, 2, 0)
-        send_last(0, (cls,))
+    send_single(0)
     for cls in range(2):
         pass_on(cls, 4, 1)
     for cls in range(2):
-        last_gram(cls, 1)
+        single_gram(cls, 1)
+        pass_on(cls, 1, 1)
         pass_on(cls, 1, 0)
-        pass_on(cls, 1, 1)
     for cls in range(2):
         pass_on(cls, 2, 1)
 
@@ -361,43 +384,54 @@
                 ] = total.astype(jnp.bfloat16)
 
     for cls in range(2):
-        last_gram(cls, 0)
+        single_gram(cls, 0)
 
     bins = bins_of(v, u, core)
-    for cls in range(2):
-        total = jnp.concatenate([gram_sum(cls, 0, piece) for piece in range(2)], axis=0)
-        high = total.astype(jnp.bfloat16)
-        low = (total - high.astype(jnp.float32)).astype(jnp.bfloat16)
-
-        def combine(straight, turned):
-            return (
-                0.5 * (straight[:64] - straight[64:] + turned[:64] + turned[64:]),
-                0.5 * (straight[:64] + straight[64:] - turned[:64] + turned[64:]),
+
+    def combine(straight, turned):
+        return (
+            0.5 * (straight[:64] - straight[64:] + turned[:64] + turned[64:]),
+            0.5 * (straight[:64] + straight[64:] - turned[:64] + turned[64:]),
+        )
+
+    def halves(whole):
+        high = whole.astype(jnp.bfloat16)
+        return high, (whole - high.astype(jnp.float32)).astype(jnp.bfloat16)
+
+    wait_sums(0)
+    both_grams = [
+        halves(jnp.concatenate([gram_sum(cls, 0, piece) for piece in range(2)], axis=0))
+        for cls in range(2)
+    ]
+    both_once = []
+    for cls in range(2):
+        (high, low), left = both_grams[cls], tmat[cls]
+        both_once.append(
+            combine(nn(left, high) + nn(left, low), nt(left, high) + nt(left, low))
+        )
+    both_twice = []
+    for cls in range(2):
+        high, low = both_grams[cls]
+        once_high, once_low = halves(jnp.concatenate(both_once[cls], axis=0))
+        lines = jnp.concatenate([once_high, once_low], axis=0)
+        straight, turned = nn(lines, high), nt(lines, high)
+        both_twice.append(
+            combine(
+                straight[:128] + straight[128:] + nn(once_high, low),
+                turned[:128] + turned[128:] + nt(once_high, low),
             )
-
-        left = tmat[cls]
-        once_re, once_im = combine(
-            nn(left, high) + nn(left, low), nt(left, high) + nt(left, low)
         )
-        once = jnp.concatenate([once_re, once_im], axis=0)
-        once_high = once.astype(jnp.bfloat16)
-        once_low = (once - once_high.astype(jnp.float32)).astype(jnp.bfloat16)
-        both = jnp.concatenate([once_high, once_low], axis=0)
-        straight, turned = nn(both, high), nt(both, high)
-        twice_re, twice_im = combine(
-            straight[:128] + straight[128:] + nn(once_high, low),
-            turned[:128] + turned[128:] + nt(once_high, low),
-        )
+    for cls in range(2):
         load = loading[bins[cls]]
         step = 1.0 / (load + rho)
         keep, take = 2.0 * step - load * step * step, step * step
-        pred = (keep * once_re - take * twice_re, keep * once_im - take * twice_im)
         for side in range(2):
+            pred = keep * both_once[cls][side] - take * both_twice[cls][side]
             for g in range(8):
                 k, tile = g % 4, g // 4
                 moved = jnp.zeros((16, 128), jnp.float32)
                 for t in range(4):
-                    turned = pred[side][t * 16 : t * 16 + 16, tile * 128 : tile * 128 + 128]
+                    turned = pred[t * 16 : t * 16 + 16, tile * 128 : tile * 128 + 128]
                     if k != t:
                         turned = pltpu.roll(turned, (32 * (t - k)) % 128, 1)
                     moved = jnp.where(lane == t, turned, moved)
@@ -406,9 +440,8 @@
     me = gx * 8 + gy
     for device in range(128):
         psend[device] = rows[device * 4 : device * 4 + 4, :].astype(jnp.bfloat16)
-    columns = [(gy + n) % 8 for n in range(8)]
-
-    def give(row, column):
+    for by_v, by_u, flip_core in FAR_FIRST:
+        row, column = place_off(by_v, by_u, flip_core)
         pltpu.make_async_remote_copy(
             src_ref=psend.at[row * 8 + column],
             dst_ref=precv.at[me],
@@ -417,15 +450,6 @@
             device_id=(row, column),
             device_id_type=MESH,
         ).start()
-
-    def give_line(n, carry):
-        for column in columns:
-            give((gx + n) % 16, column)
-        return carry
-
-    lax.fori_loop(1, 16, give_line, 0)
-    for column in columns[1:]:
-        give(gx, column)
     precv[me] = psend[me]
     wait_bytes(precv.at[pl.ds(0, 127)], p_sem.at[1])
     for device in range(128):
@@ -433,10 +457,10 @@
     out[...] = rows[...].astype(jnp.bfloat16)
 
     for cls in range(2):
-        for slot in range(3):
+        for slot in range(2):
             wait_bytes(xrecv.at[cls, slot, :, pl.ds(0, POSITIONS - 1)], x_send_sem.at[cls, slot])
-        for slot in range(2):
-            wait_bytes(xlast.at[cls, slot, :, pl.ds(0, POSITIONS - 1)], x_send_sem.at[cls, 3 + slot])
+        for slot in range(4):
+            wait_bytes(xlast.at[cls, slot, :, pl.ds(0, POSITIONS - 1)], x_send_sem.at[cls, 2 + slot])
         for piece in range(2):
             for offset in range(1, GROUPS):
                 wait_bytes(msend.at[cls, piece, offset], m_send_sem.at[cls, piece, offset])
@@ -479,10 +503,11 @@
         pltpu.VMEM((512, 512), bf16),
         pltpu.VMEM((16, 256, 512), bf16),
         pltpu.VMEM((128, 512), bf16),
+        pltpu.SMEM((256,), f32),
         pltpu.VMEM((2, CHANNELS * STRIDE, 128), f32),
         pltpu.VMEM((512, CHANNELS, 256), bf16),
-        pltpu.VMEM((2, 3, 4, POSITIONS, CHANNELS, 256), bf16),
-        pltpu.VMEM((2, 2, 2, POSITIONS, CHANNELS, 256), bf16),
+        pltpu.VMEM((2, 2, 4, POSITIONS, CHANNELS, 256), bf16),
+        pltpu.VMEM((2, 4, 2, POSITIONS, CHANNELS, 256), bf16),
         pltpu.VMEM((2, GROUPS, 256, 256), f32),
         pltpu.VMEM((2, 2, GROUPS, PIECE, 256), bf16),
         pltpu.VMEM((2, 2, GROUPS, PIECE, 256), bf16),
@@ -495,9 +520,9 @@
         pltpu.VMEM((128, 4, 128), bf16),
         pltpu.SemaphoreType.DMA((CHANNELS,)),
         pltpu.SemaphoreType.DMA((8,)),
-        pltpu.SemaphoreType.DMA((2,)),
-        pltpu.SemaphoreType.DMA((2, 5)),
-        pltpu.SemaphoreType.DMA((2, 5)),
+        pltpu.SemaphoreType.DMA((3,)),
+        pltpu.SemaphoreType.DMA((2, 6)),
+        pltpu.SemaphoreType.DMA((2, 6)),
         pltpu.SemaphoreType.DMA((2, 2, GROUPS)),
         pltpu.SemaphoreType.DMA((2, 2, GROUPS)),
         pltpu.SemaphoreType.DMA((2, 2)),
@@ -505,18 +530,18 @@
     ]
     hold = [
         pltpu.with_memory_space_constraint(array, pltpu.HBM)
-        for array in (by_pair, by_owner, proof, target.reshape(128, length))
+        for array in (by_pair, by_owner, proof, target.reshape(128, length), loading)
     ]
     spectra = pl.pallas_call(
         functools.partial(kernel, rho),
         out_shape=jax.ShapeDtypeStruct((512, 128), bf16),
-        in_specs=[hbm] * 4 + [pl.BlockSpec(memory_space=pltpu.SMEM)],
+        in_specs=[hbm] * 5,
         out_specs=pl.BlockSpec(memory_space=pltpu.VMEM),
         scratch_shapes=scratch,
         compiler_params=pltpu.CompilerParams(
             collective_id=0, has_side_effects=True, vmem_limit_bytes=40 * 2**20
         ),
-    )(*hold, loading)
+    )(*hold)
     return tn(spectra, inverse).reshape(4, 32, length)
 
 

time: 55.2 us -> 54 us (0.978)
  local copies, waits for them, and re-layouts: 0.68 us -> 0.01 us
  Pallas kernels: 53.5 us -> 52.9 us
    unnamed x4 -> x2, local copies, waits for them, and re-layouts: 0.68 us -> 0.01 us
where the time goes in v2:
time: 54 us; the launch traced here: 53.9 us
  Pallas kernels  52.9 us (98%)
  matrix products  0.96 us (2%)
    pallas_call x1, Pallas kernels, local(): pl.pallas_call(functools.partial(kernel, rho), out_shape=jax.ShapeDtypeSt...  52.9 us

profile of v2, /device:TPU:1, one launch (start us, length us, event | category | flops | bytes accessed | tf_op | source)
XLA Modules:
  0.0 53.9 jit_solution(17188844950200472118)
XLA Ops:
  0.0 0.0 copy-start
  0.0 52.9 %shard_map.64 = bf16[512,128]{1,0:T(8,128)(2,1)S(1)} custom-call(bf16[8,64,512]{2,1,0:T(8,128)(2,1)} %constant.11.tab_hbm, bf16[512,512]{1,0:T(8,128)(2,1)} %constant.12.ttab_hbm, bf16[16,256,512]{2,1,0:T(8,128)(2,1)} %proof_hbm.1, bf16[128,512]{1,0:T(8,128)(2,1)} %bitcast.4, f32[256]{0:T(256)} %loading_hbm.1), custom_call_target="tpu_custom_call" | custom-call | tf_op jit(solution)/shard_map/pallas_call | solution.py:535
  53.0 0.0 copy-done
  53.0 1.0 %fusion = f32[128,512]{1,0:T(8,128)} fusion(bf16[512,128]{1,0:T(8,128)(2,1)S(1)} %shard_map.64, bf16[512,512]{1,0:T(8,128)(2,1)S(1)} %copy-done), kind=kOutput, calls=%fused_computation | convolution fusion | flops 67108864 | bytes 917504 | tf_op jit(solution)/shard_map/dot_general | solution.py:84
Async XLA Ops:
  0.0 53.0 %copy-start = (bf16[512,512]{1,0:T(8,128)(2,1)S(1)}, bf16[512,512]{1,0:T(8,128)(2,1)}, u32[]{:S(2)}) copy-start(bf16[512,512]{1,0:T(8,128)(2,1)} %constant.13) | copy-start | bytes 1572868

commit v3 on v2

--- a/solution.py
+++ b/solution.py
@@ -13,7 +13,7 @@
 POSITIONS = 16
 CHANNELS = 16
 STRIDE = 520
-OTHERS = (2, 4, 8, 14, 3, 5, 9, 15, 6, 12, 10, 7, 13, 11, 1)
+OTHERS = (14, 12, 6, 10, 8, 4, 2, 15, 13, 7, 11, 9, 5, 3, 1)
 FAR_FIRST = sorted(
     ((v, u, core) for v in range(8) for u in range(8) for core in range(2) if v or u or core),
     key=lambda way: -(way[0].bit_count() + way[1].bit_count()),
@@ -133,19 +133,26 @@
 
     barrier = pltpu.get_barrier_semaphore()
 
+    def wait_bytes(view, sem):
+        pltpu.make_async_copy(view, view, sem).wait()
+
     def tab_copy(block):
         cls, offset = block % 2, 3 - block // 2
         return pltpu.make_async_copy(
-            tab_hbm.at[cls * 4 + pair_at(cls, offset)], tab.at[block], tab_sem.at[block]
+            tab_hbm.at[cls * 4 + pair_at(cls, offset)],
+            tab.at[block],
+            tab_sem.at[0 if block < 2 else 1],
         )
 
-    def proof_copy(c):
-        return pltpu.make_async_copy(proof_hbm.at[c], proof.at[c], proof_sem.at[c])
+    def proof_copy(c, part_of):
+        return pltpu.make_async_copy(proof_hbm.at[c], proof.at[c], proof_sem.at[part_of])
 
     for block in range(2):
         tab_copy(block).start()
-    for c in range(CHANNELS):
-        proof_copy(c).start()
+    loads = ((0, 4), (4, 8), (8, CHANNELS))
+    for part_of, (begin, end) in enumerate(loads):
+        for c in range(begin, end):
+            proof_copy(c, part_of).start()
     for block in range(2, 8):
         tab_copy(block).start()
     small = [
@@ -161,8 +168,7 @@
             pl.semaphore_signal(
                 barrier, inc=1, device_id=place(cls, other // 2, other % 2), device_id_type=MESH
             )
-    tab_copy(0).wait()
-    tab_copy(1).wait()
+    wait_bytes(tab.at[pl.ds(0, 2)], tab_sem.at[0])
 
     def spectra(begin, end, channels):
         lines = tab[begin:end].reshape((end - begin) * 64, 512)
@@ -192,7 +198,7 @@
                 pltpu.make_async_remote_copy(
                     src_ref=xsend.at[pl.ds(base[cls] + pos_at(cls, other) * 4, 4)],
                     dst_ref=xrecv.at[cls, slot, :, mine[cls]],
-                    send_sem=x_send_sem.at[cls, slot],
+                    send_sem=x_send_sem,
                     recv_sem=x_recv_sem.at[cls, slot],
                     device_id=place(cls, other // 2, other % 2),
                     device_id_type=MESH,
@@ -212,7 +218,7 @@
                 pltpu.make_async_remote_copy(
                     src_ref=xsend.at[pl.ds(base[cls] + pos_at(cls, other) * 4, 2)],
                     dst_ref=xlast.at[cls, slot, :, mine[cls]],
-                    send_sem=x_send_sem.at[cls, 2 + slot],
+                    send_sem=x_send_sem,
                     recv_sem=x_recv_sem.at[cls, 2 + slot],
                     device_id=place(cls, other // 2, other % 2),
                     device_id_type=MESH,
@@ -220,9 +226,6 @@
         for cls in classes:
             for i in range(2):
                 xlast[cls, slot, i, mine[cls]] = xsend[base[cls] + mine[cls] * 4 + i]
-
-    def wait_bytes(view, sem):
-        pltpu.make_async_copy(view, view, sem).wait()
 
     def along_positions(src, dst, sems):
         for other in OTHERS:
@@ -249,17 +252,15 @@
             ).start()
         dst[here] = src[here]
 
-    for begin, end in ((0, 4), (4, 8), (8, CHANNELS)):
-        for c in range(begin, end):
-            proof_copy(c).wait()
+    for part_of, (begin, end) in enumerate(loads):
+        wait_bytes(proof.at[pl.ds(begin, end - begin)], proof_sem.at[part_of])
         spectra(0, 2, range(begin, end))
     turn(0)
     pl.semaphore_wait(barrier, 2 * len(OTHERS))
     send_pair(3, (0,))
     turn(1)
     send_pair(3, (1,))
-    for block in range(2, 8):
-        tab_copy(block).wait()
+    wait_bytes(tab.at[pl.ds(2, 6)], tab_sem.at[1])
     spectra(2, 8, range(CHANNELS))
     turn(2)
     turn(3)
@@ -301,14 +302,19 @@
         wait_bytes(xlast.at[cls, slot, :, pl.ds(0, POSITIONS - 1)], x_recv_sem.at[cls, 2 + slot])
         part[cls, offset] = gram(xlast[cls, slot, 0], xlast[cls, slot, 1])
 
+    def sem_of(cls, offset, piece):
+        if offset == 0:
+            return m_recv_sem.at[0]
+        fed = [other for other in range(1, GROUPS) if feeders(other, piece)]
+        return m_recv_sem.at[1 + (cls * 2 + piece) * 3 + fed.index(offset)]
+
     def wait_fed(cls, offset, piece):
-        for other in feeders(offset, piece):
-            wait_bytes(mrecv.at[cls, piece, other], m_recv_sem.at[cls, piece, other])
-
-    def wait_sums(offset):
-        for cls in range(2):
-            for piece in range(2):
-                wait_fed(cls, offset, piece)
+        count = len(feeders(offset, piece))
+        if count:
+            wait_bytes(mrecv.at[cls, piece, pl.ds(0, count)], sem_of(cls, offset, piece))
+
+    def wait_sums():
+        wait_bytes(msend.at[pl.ds(0, 12)], sem_of(0, 0, 0))
 
     def gram_sum(cls, offset, piece):
         total = part[cls, offset, pl.ds(piece * PIECE, PIECE), :]
@@ -318,12 +324,13 @@
 
     def pass_on(cls, offset, piece):
         wait_fed(cls, offset, piece)
-        msend[cls, piece, offset] = gram_sum(cls, offset, piece).astype(jnp.bfloat16)
+        at = cls * 16 + piece * GROUPS + offset
+        msend[at] = gram_sum(cls, offset, piece).astype(jnp.bfloat16)
         pltpu.make_async_remote_copy(
-            src_ref=msend.at[cls, piece, offset],
+            src_ref=msend.at[at],
             dst_ref=mrecv.at[cls, piece, offset],
-            send_sem=m_send_sem.at[cls, piece, offset],
-            recv_sem=m_recv_sem.at[cls, piece, offset],
+            send_sem=m_send_sem,
+            recv_sem=sem_of(cls, offset ^ next_bit(offset, piece), piece),
             device_id=place(1 - cls, next_bit(offset, piece)),
             device_id_type=MESH,
         ).start()
@@ -398,7 +405,7 @@
         high = whole.astype(jnp.bfloat16)
         return high, (whole - high.astype(jnp.float32)).astype(jnp.bfloat16)
 
-    wait_sums(0)
+    wait_sums()
     both_grams = [
         halves(jnp.concatenate([gram_sum(cls, 0, piece) for piece in range(2)], axis=0))
         for cls in range(2)
@@ -456,14 +463,8 @@
         rows[device * 4 : device * 4 + 4, :] = precv[device].astype(jnp.float32)
     out[...] = rows[...].astype(jnp.bfloat16)
 
-    for cls in range(2):
-        for slot in range(2):
-            wait_bytes(xrecv.at[cls, slot, :, pl.ds(0, POSITIONS - 1)], x_send_sem.at[cls, slot])
-        for slot in range(4):
-            wait_bytes(xlast.at[cls, slot, :, pl.ds(0, POSITIONS - 1)], x_send_sem.at[cls, 2 + slot])
-        for piece in range(2):
-            for offset in range(1, GROUPS):
-                wait_bytes(msend.at[cls, piece, offset], m_send_sem.at[cls, piece, offset])
+    wait_bytes(xsend.at[pl.ds(0, 32 * (POSITIONS - 1))], x_send_sem)
+    wait_bytes(msend.at[pl.ds(0, 4 * (GROUPS - 1))], m_send_sem)
     wait_bytes(tpass.at[:, pl.ds(0, POSITIONS - 1)], t_sem.at[0, 0])
     wait_bytes(trecv.at[pl.ds(0, GROUPS - 1)], t_sem.at[1, 0])
     wait_bytes(precv.at[pl.ds(0, 127)], p_sem.at[0])
@@ -509,7 +510,7 @@
         pltpu.VMEM((2, 2, 4, POSITIONS, CHANNELS, 256), bf16),
         pltpu.VMEM((2, 4, 2, POSITIONS, CHANNELS, 256), bf16),
         pltpu.VMEM((2, GROUPS, 256, 256), f32),
-        pltpu.VMEM((2, 2, GROUPS, PIECE, 256), bf16),
+        pltpu.VMEM((4 * GROUPS, PIECE, 256), bf16),
         pltpu.VMEM((2, 2, GROUPS, PIECE, 256), bf16),
         pltpu.VMEM((2, 128, 256), bf16),
         pltpu.VMEM((POSITIONS, GROUPS, 4, 128), bf16),
@@ -518,13 +519,13 @@
         pltpu.VMEM((512, 128), f32),
         pltpu.VMEM((128, 4, 128), bf16),
         pltpu.VMEM((128, 4, 128), bf16),
-        pltpu.SemaphoreType.DMA((CHANNELS,)),
-        pltpu.SemaphoreType.DMA((8,)),
         pltpu.SemaphoreType.DMA((3,)),
+        pltpu.SemaphoreType.DMA((2,)),
+        pltpu.SemaphoreType.DMA((3,)),
+        pltpu.SemaphoreType.DMA,
         pltpu.SemaphoreType.DMA((2, 6)),
-        pltpu.SemaphoreType.DMA((2, 6)),
-        pltpu.SemaphoreType.DMA((2, 2, GROUPS)),
-        pltpu.SemaphoreType.DMA((2, 2, GROUPS)),
+        pltpu.SemaphoreType.DMA,
+        pltpu.SemaphoreType.DMA((13,)),
         pltpu.SemaphoreType.DMA((2, 2)),
         pltpu.SemaphoreType.DMA((2,)),
     ]

time: 54 us -> 51.6 us (0.956)
  Pallas kernels: 52.9 us -> 50.6 us
    pallas_call x1, Pallas kernels: 52.9 us -> 50.6 us  [local(): pl.pallas_call(functools.partial(kernel, rho), out_shape=jax.ShapeDtypeSt...]
where the time goes in v3:
time: 51.6 us; the launch traced here: 51.5 us
  Pallas kernels  50.6 us (98%)
  matrix products  0.96 us (2%)
    pallas_call x1, Pallas kernels, local(): pl.pallas_call(functools.partial(kernel, rho), out_shape=jax.ShapeDtypeSt...  50.6 us

profile of v3, /device:TPU:1, one launch (start us, length us, event | category | flops | bytes accessed | tf_op | source)
XLA Modules:
  0.0 51.5 jit_solution(4862047856752456013)
XLA Ops:
  0.0 0.0 copy-start
  0.0 50.6 %shard_map.64 = bf16[512,128]{1,0:T(8,128)(2,1)S(1)} custom-call(bf16[8,64,512]{2,1,0:T(8,128)(2,1)} %constant.11.tab_hbm, bf16[512,512]{1,0:T(8,128)(2,1)} %constant.12.ttab_hbm, bf16[16,256,512]{2,1,0:T(8,128)(2,1)} %proof_hbm.1, bf16[128,512]{1,0:T(8,128)(2,1)} %bitcast.4, f32[256]{0:T(256)} %loading_hbm.1), custom_call_target="tpu_custom_call" | custom-call | tf_op jit(solution)/shard_map/pallas_call | solution.py:536
  50.6 0.0 copy-done
  50.6 1.0 %fusion = f32[128,512]{1,0:T(8,128)} fusion(bf16[512,128]{1,0:T(8,128)(2,1)S(1)} %shard_map.64, bf16[512,512]{1,0:T(8,128)(2,1)S(1)} %copy-done), kind=kOutput, calls=%fused_computation | convolution fusion | flops 67108864 | bytes 917504 | tf_op jit(solution)/shard_map/dot_general | solution.py:84
Async XLA Ops:
  0.0 50.6 %copy-start = (bf16[512,512]{1,0:T(8,128)(2,1)S(1)}, bf16[512,512]{1,0:T(8,128)(2,1)}, u32[]{:S(2)}) copy-start(bf16[512,512]{1,0:T(8,128)(2,1)} %constant.13) | copy-start | bytes 1572868

commit v4 on v3

--- a/solution.py
+++ b/solution.py
@@ -149,7 +149,7 @@
 
     for block in range(2):
         tab_copy(block).start()
-    loads = ((0, 4), (4, 8), (8, CHANNELS))
+    loads = ((0, 6), (6, CHANNELS))
     for part_of, (begin, end) in enumerate(loads):
         for c in range(begin, end):
             proof_copy(c, part_of).start()
@@ -297,10 +297,17 @@
                 xrecv[cls, slot, row], xrecv[cls, slot, row + 1]
             )
 
-    def single_gram(cls, offset):
+    def wait_single(cls, offset):
         slot = 3 - offset
         wait_bytes(xlast.at[cls, slot, :, pl.ds(0, POSITIONS - 1)], x_recv_sem.at[cls, 2 + slot])
+
+    def arrived_gram(cls, offset):
+        slot = 3 - offset
         part[cls, offset] = gram(xlast[cls, slot, 0], xlast[cls, slot, 1])
+
+    def single_gram(cls, offset):
+        wait_single(cls, offset)
+        arrived_gram(cls, offset)
 
     def sem_of(cls, offset, piece):
         if offset == 0:
@@ -391,7 +398,9 @@
                 ] = total.astype(jnp.bfloat16)
 
     for cls in range(2):
-        single_gram(cls, 0)
+        wait_single(cls, 0)
+    for cls in range(2):
+        arrived_gram(cls, 0)
 
     bins = bins_of(v, u, core)
 

time: 51.6 us -> 51.5 us (level)
  no operation moved by 1% of the time
where the time goes in v4:
time: 51.5 us; the launch traced here: 51.4 us
  Pallas kernels  50.4 us (98%)
  matrix products  0.96 us (2%)
    pallas_call x1, Pallas kernels, local(): pl.pallas_call(functools.partial(kernel, rho), out_shape=jax.ShapeDtypeSt...  50.4 us

profile of v4, /device:TPU:1, one launch (start us, length us, event | category | flops | bytes accessed | tf_op | source)
XLA Modules:
  0.0 51.4 jit_solution(16978652787054265267)
XLA Ops:
  0.0 0.0 copy-start
  0.0 50.4 %shard_map.64 = bf16[512,128]{1,0:T(8,128)(2,1)S(1)} custom-call(bf16[8,64,512]{2,1,0:T(8,128)(2,1)} %constant.11.tab_hbm, bf16[512,512]{1,0:T(8,128)(2,1)} %constant.12.ttab_hbm, bf16[16,256,512]{2,1,0:T(8,128)(2,1)} %proof_hbm.1, bf16[128,512]{1,0:T(8,128)(2,1)} %bitcast.4, f32[256]{0:T(256)} %loading_hbm.1), custom_call_target="tpu_custom_call" | custom-call | tf_op jit(solution)/shard_map/pallas_call | solution.py:545
  50.4 0.0 copy-done
  50.4 1.0 %fusion = f32[128,512]{1,0:T(8,128)} fusion(bf16[512,128]{1,0:T(8,128)(2,1)S(1)} %shard_map.64, bf16[512,512]{1,0:T(8,128)(2,1)S(1)} %copy-done), kind=kOutput, calls=%fused_computation | convolution fusion | flops 67108864 | bytes 917504 | tf_op jit(solution)/shard_map/dot_general | solution.py:84
Async XLA Ops:
  0.0 50.4 %copy-start = (bf16[512,512]{1,0:T(8,128)(2,1)S(1)}, bf16[512,512]{1,0:T(8,128)(2,1)}, u32[]{:S(2)}) copy-start(bf16[512,512]{1,0:T(8,128)(2,1)} %constant.13) | copy-start | bytes 1572868

commit v5 on v4

--- a/solution.py
+++ b/solution.py
@@ -150,9 +150,17 @@
     for block in range(2):
         tab_copy(block).start()
     loads = ((0, 6), (6, CHANNELS))
-    for part_of, (begin, end) in enumerate(loads):
-        for c in range(begin, end):
-            proof_copy(c, part_of).start()
+    for c in range(*loads[0]):
+        proof_copy(c, 0).start()
+
+    for other in OTHERS:
+        for cls in range(2):
+            pl.semaphore_signal(
+                barrier, inc=1, device_id=place(cls, other // 2, other % 2), device_id_type=MESH
+            )
+
+    for c in range(*loads[1]):
+        proof_copy(c, 1).start()
     for block in range(2, 8):
         tab_copy(block).start()
     small = [
@@ -163,11 +171,6 @@
     for copy in small:
         copy.start()
 
-    for other in OTHERS:
-        for cls in range(2):
-            pl.semaphore_signal(
-                barrier, inc=1, device_id=place(cls, other // 2, other % 2), device_id_type=MESH
-            )
     wait_bytes(tab.at[pl.ds(0, 2)], tab_sem.at[0])
 
     def spectra(begin, end, channels):

time: 51.5 us -> 51.6 us (level)
  no operation moved by 1% of the time
where the time goes in v5:
time: 51.6 us; the launch traced here: 51.5 us
  Pallas kernels  50.5 us (98%)
  matrix products  0.96 us (2%)
    pallas_call x1, Pallas kernels, local(): pl.pallas_call(functools.partial(kernel, rho), out_shape=jax.ShapeDtypeSt...  50.5 us

profile of v5, /device:TPU:1, one launch (start us, length us, event | category | flops | bytes accessed | tf_op | source)
XLA Modules:
  0.0 51.5 jit_solution(18390644942409205438)
XLA Ops:
  0.0 0.0 copy-start
  0.0 50.5 %shard_map.64 = bf16[512,128]{1,0:T(8,128)(2,1)S(1)} custom-call(bf16[8,64,512]{2,1,0:T(8,128)(2,1)} %constant.11.tab_hbm, bf16[512,512]{1,0:T(8,128)(2,1)} %constant.12.ttab_hbm, bf16[16,256,512]{2,1,0:T(8,128)(2,1)} %proof_hbm.1, bf16[128,512]{1,0:T(8,128)(2,1)} %bitcast.4, f32[256]{0:T(256)} %loading_hbm.1), custom_call_target="tpu_custom_call" | custom-call | tf_op jit(solution)/shard_map/pallas_call | solution.py:548
  50.5 0.0 copy-done
  50.5 1.0 %fusion = f32[128,512]{1,0:T(8,128)} fusion(bf16[512,128]{1,0:T(8,128)(2,1)S(1)} %shard_map.64, bf16[512,512]{1,0:T(8,128)(2,1)S(1)} %copy-done), kind=kOutput, calls=%fused_computation | convolution fusion | flops 67108864 | bytes 917504 | tf_op jit(solution)/shard_map/dot_general | solution.py:84
Async XLA Ops:
  0.0 50.5 %copy-start = (bf16[512,512]{1,0:T(8,128)(2,1)S(1)}, bf16[512,512]{1,0:T(8,128)(2,1)}, u32[]{:S(2)}) copy-start(bf16[512,512]{1,0:T(8,128)(2,1)} %constant.13) | copy-start | bytes 1572868
